TPU v7x, 32 devices: a whole 2x2x4 slice. The times are simulated.
32 devices in a mesh: seq: 2 (over core), width: 4 (over y, x), dp: 4 (over z).
Axes of the slice: x: 2, y: 2, z: 4, core: 2. Of those that a mesh axis runs over, the one named last changes fastest.
Arguments:
- inputs: bfloat16 [4, 512, 5376], P('dp', 'seq', 'width'), may hold values from -6 to 6
- out_grad: bfloat16 [4, 512, 5376], P('dp', 'seq', 'width'), may hold values from -6 to 6
- gate_a: bfloat16 [16, 336, 336], P('width'), may hold values from -0.3125 to 0.3125
- gate_x: bfloat16 [16, 336, 336], P('width'), may hold values from -0.3125 to 0.3125
- bias_a: float32 [5376], P('width'), may hold values from -1.5 to 1.5
- bias_x: float32 [5376], P('width'), may hold values from -1.5 to 1.5
- decay_param: float32 [5376], P('width'), may hold values from -12 to -4.5
- segment_ids: int32 [4, 512], P('dp', 'seq'), may hold values from 0 to 3, never falling along the last dimension, each value on 1 to 256 neighbouring positions
Outputs:
- input_grad: bfloat16 [4, 512, 5376], P('dp', 'seq', 'width')
- gate_a_grad: float32 [16, 336, 336], P('width')
- gate_x_grad: float32 [16, 336, 336], P('width')
- bias_a_grad: float32 [5376], P('width')
- bias_x_grad: float32 [5376], P('width')
- decay_grad: float32 [5376], P('width')
All inputs are finite; a program needn't handle non-finite values.
Results may differ from a plain program's by a relative error of at most 0.0029.
Values sent between devices are 32-bit elements; how exact they have to be, the bound alone decides.
No kernel may reach another device: no remote copies, remote signals or barrier semaphores. Data moves between devices by JAX's collectives and lax.ppermute only.
A program may use at most 128 MiB of HBM per device.

v0:
```python
import jax
import jax.numpy as jnp
from jax import lax
from jax.sharding import PartitionSpec as P


def shifted(value, axis, steps):
    count = lax.axis_size(axis)
    initial, last = (max(0, -steps), min(count, count - steps))
    return lax.ppermute(value, axis, [(source, source + steps) for source in range(initial, last)])


def carried_in(value, axis, join, neutral, backward):
    count, mine = (lax.axis_size(axis), lax.axis_index(axis))
    pieces = jax.tree.map(lambda part: lax.all_gather(part, axis), value)
    if backward:
        pieces = jax.tree.map(lambda part: part[::-1], pieces)
        mine = count - 1 - mine
    running = jax.tree.map(
        lambda part, zero: jnp.full_like(part, 0) + jnp.asarray(zero, part.dtype), value, neutral
    )

    def hop(position, running):
        longer = join(running, jax.tree.map(lambda part: part[position], pieces))
        return jax.tree.map(lambda new, old: jnp.where(position < mine, new, old), longer, running)

    return lax.fori_loop(0, count - 1, hop, running)


def combine(earlier, later):
    return (earlier[0] * later[0], earlier[1] * later[0] + later[1])


def shards(inputs, out_grad, gate_a, gate_x, bias_a, bias_x, decay_param, segment_ids):
    batch, count, chans = inputs.shape
    blocks, width_k = (gate_a.shape[0], gate_a.shape[1])
    span_len = 8
    groups = count // span_len
    blocked = inputs.reshape(batch, count, blocks, width_k)
    pre_a = (
        jnp.einsum("stbk,bkj->stbj", blocked, gate_a, preferred_element_type=jnp.float32).reshape(
            batch, count, chans
        )
        + bias_a
    )
    pre_x = (
        jnp.einsum("stbk,bkj->stbj", blocked, gate_x, preferred_element_type=jnp.float32).reshape(
            batch, count, chans
        )
        + bias_x
    )
    rate = jax.nn.sigmoid(pre_a)
    ingate = jax.nn.sigmoid(pre_x)
    soft = jax.nn.softplus(decay_param)
    log_a = -8.0 * rate * soft
    decay = jnp.exp(log_a)
    shifted_ids = segment_ids + 1
    before = shifted(shifted_ids[:, -1:], "seq", 1)
    previous = jnp.concatenate([before, shifted_ids[:, :-1]], 1)
    position = lax.axis_index("seq") * count + jnp.arange(count, dtype=jnp.int32)
    reset = (shifted_ids != previous) | (position[None, :] == 0)
    keep = jnp.where(reset, 0.0, 1.0).astype(jnp.float32)[:, :, None]
    abar = keep * decay
    mult = jnp.where(keep > 0.5, jnp.sqrt(-jnp.expm1(2.0 * log_a)), 1.0)
    xf = inputs.astype(jnp.float32)
    dyf = out_grad.astype(jnp.float32)
    drive = mult * ingate * xf
    cum_log = jnp.cumsum(log_a.reshape(batch, groups, span_len, chans), 2)
    cum_reset = jnp.cumsum(
        jnp.where(reset, 1.0, 0.0).astype(jnp.float32).reshape(batch, groups, span_len), 2
    )
    order = jnp.arange(span_len, dtype=jnp.int32)
    lower = order[:, None] >= order[None, :]
    linked = (cum_reset[:, :, :, None] == cum_reset[:, :, None, :]) & lower
    spread = cum_log[:, :, :, None, :] - cum_log[:, :, None, :, :]
    factor = jnp.where(linked[..., None], jnp.exp(jnp.minimum(spread, 0.0)), 0.0)
    state_loc = jnp.einsum(
        "bntsc,bnsc->bntc",
        factor,
        drive.reshape(batch, groups, span_len, chans),
        precision=lax.Precision.HIGHEST,
    )
    grad_loc = jnp.einsum(
        "bntsc,bntc->bnsc",
        factor,
        dyf.reshape(batch, groups, span_len, chans),
        precision=lax.Precision.HIGHEST,
    )
    from_start = jnp.exp(cum_log) * jnp.where(cum_reset == 0.0, 1.0, 0.0)[..., None]
    to_end = (
        jnp.exp(cum_log[:, :, -1:, :] - cum_log)
        * jnp.where(cum_reset == cum_reset[:, :, -1:], 1.0, 0.0)[..., None]
    )
    group_prod = from_start[:, :, -1]
    group_state = state_loc[:, :, -1]
    group_grad = abar.reshape(batch, groups, span_len, chans)[:, :, 0] * grad_loc[:, :, 0]
    fwd_p, fwd_s = lax.associative_scan(combine, (group_prod, group_state), axis=1)
    bwd_p, bwd_s = lax.associative_scan(combine, (group_prod, group_grad), reverse=True, axis=1)
    forward_sum = (fwd_p[:, -1], fwd_s[:, -1])
    backward_sum = (bwd_p[:, 0], bwd_s[:, 0])
    unit = jnp.ones((batch, chans), jnp.float32)
    naught = jnp.zeros((batch, chans), jnp.float32)
    state_in = carried_in(forward_sum, "seq", combine, (unit, naught), False)[1]
    grad_in = carried_in(backward_sum, "seq", combine, (unit, naught), True)[1]
    excl_p = jnp.concatenate([unit[:, None], fwd_p[:, :-1]], 1)
    excl_s = jnp.concatenate([naught[:, None], fwd_s[:, :-1]], 1)
    entering = excl_s + excl_p * state_in[:, None, :]
    later_p = jnp.concatenate([bwd_p[:, 1:], unit[:, None]], 1)
    later_s = jnp.concatenate([bwd_s[:, 1:], naught[:, None]], 1)
    leaving = later_s + later_p * grad_in[:, None, :]
    state = (state_loc + from_start * entering[:, :, None, :]).reshape(batch, count, chans)
    grad = (grad_loc + to_end * leaving[:, :, None, :]).reshape(batch, count, chans)
    wsum = grad * (state - drive) - keep * (grad * ingate * xf * decay * decay / mult)
    dpre_a = -8.0 * soft * rate * (1.0 - rate) * wsum
    dpre_x = grad * mult * xf * ingate * (1.0 - ingate)
    da_b = dpre_a.astype(jnp.bfloat16).reshape(batch, count, blocks, width_k)
    dx_b = dpre_x.astype(jnp.bfloat16).reshape(batch, count, blocks, width_k)
    back = jnp.einsum(
        "stbj,bkj->stbk", da_b, gate_a, preferred_element_type=jnp.float32
    ) + jnp.einsum("stbj,bkj->stbk", dx_b, gate_x, preferred_element_type=jnp.float32)
    input_grad = (grad * mult * ingate + back.reshape(batch, count, chans)).astype(jnp.bfloat16)
    local_a = jnp.einsum("stbk,stbj->bkj", blocked, da_b, preferred_element_type=jnp.float32)
    local_x = jnp.einsum("stbk,stbj->bkj", blocked, dx_b, preferred_element_type=jnp.float32)
    bias_ga = jnp.sum(dpre_a, (0, 1))
    bias_gx = jnp.sum(dpre_x, (0, 1))
    decay_g = jnp.sum(-8.0 * rate * wsum, (0, 1))
    grad_a, grad_x, bias_ga, bias_gx, decay_g = lax.psum(
        (local_a, local_x, bias_ga, bias_gx, decay_g), ("seq", "dp")
    )
    return (input_grad, grad_a, grad_x, bias_ga, bias_gx, jax.nn.sigmoid(decay_param) * decay_g)


def solution(mesh):
    in_specs = (
        P("dp", "seq", "width"),
        P("dp", "seq", "width"),
        P("width", None, None),
        P("width", None, None),
        P("width"),
        P("width"),
        P("width"),
        P("dp", "seq"),
    )
    out_specs = (
        P("dp", "seq", "width"),
        P("width", None, None),
        P("width", None, None),
        P("width"),
        P("width"),
        P("width"),
    )
    return jax.shard_map(shards, mesh=mesh, in_specs=in_specs, out_specs=out_specs, check_vma=False)
```

profile of v0, /device:TPU:0, one launch (start us, length us, event | category | flops | bytes accessed | tf_op | source)
XLA Modules:
  0.0 415.5 jit_solution(12818486162488649593)
XLA Ops:
  8.6 2.9 collective-permute-start
  12.2 2.3 copy.78
  19.0 2.9 copy.77
  25.0 2.1 reshape.984
  28.6 6.4 %reduce_window_sum.23 = f32[1,32,8,1344]{3,2,1,0:T(8,128)S(1)} reduce-window(f32[1,32,8,1344]{3,2,1,0:T(8,128)} %divide_multiply_fusion, f32[]{:T(128)} %constant.20.clone.1), window={size=1x1x8x1 pad=0_0x0_0x7_0x0_0}, to_apply=%region_1.2 | reduce-window | flops 2408448 | bytes 2752516 | tf_op jit(solution)/shard_map/jit(cumsum)/reduce_window_sum | solution.py:68
  37.2 4.8 %multiply_reduce_fusion.1 = f32[32,1344,8]{1,2,0:T(8,128)S(1)} fusion(f32[32,1344,8]{1,2,0:T(8,128)} %bitcast_convert_fusion, f32[32,8,1344]{2,1,0:T(8,128)S(1)} %bitcast.111, pred[32,8,8]{2,1,0:T(8,128)(4,1)S(1)} %compare_and_fusion), kind=kLoop, calls=%fused_computation.1 | loop fusion | flops 13418496 | bytes 4130816 | tf_op jit(solution)/shard_map/bntsc,bntc->bnsc/dot_general | solution.py:83
  47.9 15.7 %multiply_reduce_fusion = f32[32,1344,8]{1,2,0:T(8,128)S(1)} fusion(f32[32,1344,8]{1,2,0:T(8,128)S(1)} %fusion.6, f32[32,8,1344]{2,1,0:T(8,128)S(1)} %bitcast.112, pred[32,8,8]{2,1,0:T(8,128)(4,1)S(1)} %compare_and_fusion), kind=kLoop, calls=%fused_computation | loop fusion | flops 13418496 | bytes 4130816 | tf_op jit(solution)/shard_map/bntsc,bnsc->bntc/dot_general | solution.py:77
  87.1 3.2 pad.142
  91.6 3.2 pad.132
  94.8 3.2 pad.133
  98.0 3.2 pad.143
  113.1 1.9 pad.150
  116.9 1.9 pad.161
  120.2 1.9 pad.160
  127.6 3.2 pad.162
  132.2 3.2 pad.152
  135.4 3.2 pad.153
  138.6 3.2 pad.163
  147.7 4.7 %pad.164 = f32[1,16,1344]{2,0,1:T(1,128)} pad(f32[1,8,1344]{2,0,1:T(1,128)} %pad_maximum_fusion.7, f32[]{:T(128)} %constant.20.clone.1), padding=0_0_0x0_1_1x0_0_0 | pad | bytes 129028 | tf_op jit(solution)/shard_map/pad | solution.py:97
  153.8 4.7 %pad.154 = f32[1,16,1344]{2,0,1:T(1,128)} pad(f32[1,8,1344]{2,0,1:T(1,128)} %pad_maximum_fusion.6, f32[]{:T(128)} %constant.20.clone.1), padding=0_0_0x0_1_1x0_0_0 | pad | bytes 129028 | tf_op jit(solution)/shard_map/pad | solution.py:97
  158.4 4.7 %pad.155 = f32[1,16,1344]{2,0,1:T(1,128)} pad(f32[1,8,1344]{2,0,1:T(1,128)} %add.512, f32[]{:T(128)} %constant.20.clone.1), padding=0_0_0x1_0_1x0_0_0 | pad | bytes 129028 | tf_op jit(solution)/shard_map/pad | solution.py:97
  163.1 4.7 %pad.165 = f32[1,16,1344]{2,0,1:T(1,128)} pad(f32[1,8,1344]{2,0,1:T(1,128)} %add.519, f32[]{:T(128)} %constant.20.clone.1), padding=0_0_0x1_0_1x0_0_0 | pad | bytes 129028 | tf_op jit(solution)/shard_map/pad | solution.py:97
  169.4 2.0 fusion.34
  172.4 5.6 %pad.307 = f32[1,31,1344]{2,0,1:T(1,128)} pad(f32[1,16,1344]{2,0,1:T(1,128)S(1)} %add.520, f32[]{:T(128)} %constant.20.clone.1), padding=0_0_0x0_0_1x0_0_0 | pad | bytes 252676
  178.0 5.6 %pad.167 = f32[1,32,1344]{2,0,1:T(1,128)} pad(f32[1,16,1344]{2,0,1:T(1,128)S(1)} %add.520, f32[]{:T(128)} %constant.20.clone.1), padding=0_0_0x1_0_1x0_0_0 | pad | bytes 258052 | tf_op jit(solution)/shard_map/pad | solution.py:97
  183.5 8.4 %pad.305 = f32[1,31,1344]{2,0,1:T(1,128)} pad(f32[1,16,1344]{2,0,1:T(1,128)} %add.514, f32[]{:T(128)} %constant.20.clone.1), padding=0_0_0x0_0_1x0_0_0 | pad | bytes 252676
  192.0 8.4 %pad.157 = f32[1,32,1344]{2,0,1:T(1,128)} pad(f32[1,16,1344]{2,0,1:T(1,128)} %add.514, f32[]{:T(128)} %constant.20.clone.1), padding=0_0_0x1_0_1x0_0_0 | pad | bytes 258052 | tf_op jit(solution)/shard_map/pad | solution.py:97
  201.7 5.6 %pad.309 = f32[1,31,1344]{2,0,1:T(1,128)} pad(f32[1,16,1344]{2,0,1:T(1,128)S(1)} %add.486, f32[]{:T(128)} %constant.20.clone.1), padding=0_0_0x0_0_1x0_0_0 | pad | bytes 252676
  207.2 5.5 %pad.137 = f32[1,32,1344]{2,0,1:T(1,128)} pad(f32[1,16,1344]{2,0,1:T(1,128)S(1)} %add.486, f32[]{:T(128)} %constant.20.clone.1), padding=0_0_0x1_0_1x0_0_0 | pad | bytes 258052 | tf_op jit(solution)/shard_map/pad | solution.py:98
  213.7 4.7 %pad.145 = f32[1,16,1344]{2,0,1:T(1,128)} pad(f32[1,8,1344]{2,0,1:T(1,128)} %add.491, f32[]{:T(128)} %constant.20.clone.1), padding=0_0_0x1_0_1x0_0_0 | pad | bytes 129028 | tf_op jit(solution)/shard_map/pad | solution.py:98
  219.4 5.6 %pad.311 = f32[1,31,1344]{2,0,1:T(1,128)} pad(f32[1,16,1344]{2,0,1:T(1,128)S(1)} %add.492, f32[]{:T(128)} %constant.20.clone.1), padding=0_0_0x0_0_1x0_0_0 | pad | bytes 252676
  225.0 5.6 %pad.147 = f32[1,32,1344]{2,0,1:T(1,128)} pad(f32[1,16,1344]{2,0,1:T(1,128)S(1)} %add.492, f32[]{:T(128)} %constant.20.clone.1), padding=0_0_0x1_0_1x0_0_0 | pad | bytes 258052 | tf_op jit(solution)/shard_map/pad | solution.py:98
  231.5 5.6 %pad.156 = f32[1,32,1344]{2,0,1:T(1,128)} pad(f32[1,16,1344]{2,0,1:T(1,128)S(1)} %pad_maximum_fusion.2, f32[]{:T(128)} %constant.20.clone.1), padding=0_0_0x0_1_1x0_0_0 | pad | bytes 258052 | tf_op jit(solution)/shard_map/pad | solution.py:97
  238.1 5.5 %pad.166 = f32[1,32,1344]{2,0,1:T(1,128)} pad(f32[1,16,1344]{2,0,1:T(1,128)S(1)} %pad_maximum_fusion.3, f32[]{:T(128)} %constant.20.clone.1), padding=0_0_0x0_1_1x0_0_0 | pad | bytes 258052 | tf_op jit(solution)/shard_map/pad | solution.py:97
  246.9 8.5 %pad.146 = f32[1,32,1344]{2,0,1:T(1,128)} pad(f32[1,16,1344]{2,0,1:T(1,128)} %pad_maximum_fusion.1, f32[]{:T(128)} %constant.20.clone.1), padding=0_0_0x0_1_1x0_0_0 | pad | bytes 258052 | tf_op jit(solution)/shard_map/pad | solution.py:98
  257.0 8.4 %pad.136 = f32[1,32,1344]{2,0,1:T(1,128)} pad(f32[1,16,1344]{2,0,1:T(1,128)} %pad_maximum_fusion, f32[]{:T(128)} %constant.20.clone.1), padding=0_0_0x0_1_1x0_0_0 | pad | bytes 258052 | tf_op jit(solution)/shard_map/pad | solution.py:98
  269.6 1.9 all_gather.12
  271.6 1.9 all_gather.13
  284.3 7.3 %fusion.15 = (f32[1344]{0:T(1024)}, f32[1,256,1344]{2,1,0:T(8,128)S(1)}, f32[1344]{0:T(1024)}, f32[1344]{0:T(1024)}, f32[1,256,1344]{2,1,0:T(8,128)}) fusion(bf16[1,256,1344]{2,1,0:T(8,128)(2,1)} %copy.78, f32[1,256,1344]{2,1,0:T(8,128)} %copy.77, f32[1344]{0:T(1024)} %param.13, f32[1344]{0:T(1024)S(1)} %fusion.19, f32[1,256,1344]{2,1,0:T(8,128)} %copy.75, ...), kind=kLoop, calls=%fused_computation.84 | loop fusion | flops 15134784 | bytes 10873600 | tf_op jit(solution)/shard_map/reduce_sum | solution.py:125
  294.0 2.2 copy.82
  296.3 2.7 fusion.8
  306.9 3.1 copy.83
  310.0 3.3 add_convert_fusion
  313.3 2.2 copy.84
  315.6 33.0 %all-reduce.44 = (f32[1344]{0:T(1024)}, f32[1344]{0:T(1024)}, f32[1344]{0:T(1024)S(1)}) all-reduce(f32[1344]{0:T(1024)S(1)} %copy-done.35, f32[1344]{0:T(1024)S(1)} %copy-done.34, f32[1344]{0:T(1024)S(1)} %copy-done.36), channel_id=1, replica_groups=mesh['seq'=2,'width'=4,'dp'=4] {'seq','dp'}, use_global_device_ids=true, to_apply=%region_5.6 | all-reduce | flops 4032 | bytes 32256 | tf_op jit(solution)/shard_map/psum | solution.py:127
  349.2 53.6 %all-reduce.48.cloned.1.call-done = (f32[4,336,336]{1,2,0:T(8,128)}, f32[4,336,336]{1,2,0:T(8,128)}) async-done(((f32[4,336,336]{1,2,0:T(8,128)}, f32[4,336,336]{1,2,0:T(8,128)}), (f32[4,336,336]{1,2,0:T(8,128)}, f32[4,336,336]{1,2,0:T(8,128)})) %all-reduce.48.cloned.1.call-update) | async-done | bytes 3612688 | tf_op jit(solution)/shard_map/psum | solution.py:127
  402.8 2.9 copy.85
  405.7 2.9 copy.86
  (208 shorter events, 111.7 us)
Async XLA Ops:
  7.2 8.9 %copy-start = (bf16[4,336,336]{2,1,0:T(8,128)(2,1)S(1)}, bf16[4,336,336]{2,1,0:T(8,128)(2,1)}, u32[]{:S(2)}) copy-start(bf16[4,336,336]{2,1,0:T(8,128)(2,1)} %param.10) | copy-start | bytes 2709508
  7.2 7.3 %copy-start.21 = (bf16[1,256,1344]{1,2,0:T(8,128)(2,1)S(1)}, bf16[1,256,1344]{1,2,0:T(8,128)(2,1)}, u32[]{:S(2)}) copy-start(bf16[1,256,1344]{1,2,0:T(8,128)(2,1)} %param.9) | copy-start | bytes 2064388
  7.2 395.6 %all-reduce.48.cloned.1.call-start = ((), (), s32[]{:S(2)}) async-start(), calls=%async_computation | async-start | bytes 8257536 | tf_op jit(solution)/shard_map/psum | solution.py:127
  8.6 27.3 %collective-permute-start = (s32[1,1]{1,0:T(1,128)}, s32[1,1]{1,0:T(1,128)}, u32[]{:S(2)}, u32[]{:S(2)}) collective-permute-start(s32[1,1]{1,0:T(1,128)} %slice.468), channel_id=1, source_target_pairs={{0,16},{1,17},{2,18},{3,19},{4,20},{5,21},{6,22},{7,23},{8,24},{9,... | collective-permute-start | bytes 20 | tf_op jit(solution)/shard_map/ppermute | solution.py:10
  14.5 1.6 copy-start.6
  16.1 1.2 copy-start.13
  25.0 2.1 copy-start.29
  28.6 7.3 %copy-start.41 = (s32[1,256]{1,0:T(1,128)S(1)}, s32[1,256]{1,0:T(1,128)}, u32[]{:S(2)}) copy-start(s32[1,256]{1,0:T(1,128)} %param.15) | copy-start | bytes 3076
  36.5 9.0 %copy-start.40 = (f32[1,256]{1,0:T(1,128)}, f32[1,256]{1,0:T(1,128)S(1)}, u32[]{:S(2)}) copy-start(f32[1,256]{1,0:T(1,128)S(1)} %get-tuple-element.78) | copy-start | bytes 3076
  37.2 9.1 %copy-start.1 = (f32[1,256,1344]{2,1,0:T(8,128)S(1)}, f32[1,256,1344]{2,1,0:T(8,128)}, u32[]{:S(2)}) copy-start(f32[1,256,1344]{2,1,0:T(8,128)} %copy.77) | copy-start | bytes 4128772
  37.2 9.1 %copy-start.4 = (f32[1,256,1344]{2,1,0:T(8,128)S(1)}, f32[1,256,1344]{2,1,0:T(8,128)}, u32[]{:S(2)}) copy-start(f32[1,256,1344]{2,1,0:T(8,128)} %copy.75) | copy-start | bytes 4128772
  37.2 9.1 %copy-start.31 = (f32[1344]{0:T(1024)S(1)}, f32[1344]{0:T(1024)}, u32[]{:S(2)}) copy-start(f32[1344]{0:T(1024)} %param.13) | copy-start | bytes 16132
  42.0 1.1 copy-start.10
  42.0 4.3 %copy-start.8 = (bf16[1,256,1344]{2,1,0:T(8,128)(2,1)S(1)}, bf16[1,256,1344]{2,1,0:T(8,128)(2,1)}, u32[]{:S(2)}) copy-start(bf16[1,256,1344]{2,1,0:T(8,128)(2,1)} %copy.78) | copy-start | bytes 2064388
  44.8 3.1 copy-start.15
  45.6 2.3 copy-start.42
  63.7 1.1 copy-start.11
  67.5 1.2 copy-start.22
  67.5 1.3 copy-start.23
  68.8 1.2 copy-start.24
  68.8 1.3 copy-start.25
  109.3 1.2 copy-start.26
  109.3 1.3 copy-start.27
  112.5 39.9 %copy-start.39 = (f32[1,1,1344]{2,0,1:T(1,128)S(1)}, f32[1,1,1344]{2,0,1:T(1,128)}, u32[]{:S(2)}) copy-start(f32[1,1,1344]{2,0,1:T(1,128)} %slice.512) | copy-start | bytes 16132
  171.4 30.0 %copy-start.28 = (f32[1,8,1344]{2,0,1:T(1,128)S(1)}, f32[1,8,1344]{2,0,1:T(1,128)}, u32[]{:S(2)}) copy-start(f32[1,8,1344]{2,0,1:T(1,128)} %add.484) | copy-start | bytes 129028
  171.4 41.4 %copy-start.38 = (f32[1,1,1344]{2,0,1:T(1,128)S(1)}, f32[1,1,1344]{2,0,1:T(1,128)}, u32[]{:S(2)}) copy-start(f32[1,1,1344]{2,0,1:T(1,128)} %slice.496) | copy-start | bytes 16132
  218.4 36.9 %slice-start = ((f32[1,32,1344]{2,0,1:T(1,128)}), f32[1,1,1344]{2,0,1:T(1,128)S(1)}, s32[]{:S(2)}) async-start(f32[1,32,1344]{2,0,1:T(1,128)} %copy-done.15), calls=%async_computation.1 | async-start | bytes 11264 | tf_op jit(solution)/shard_map/slice | solution.py:98
  245.4 31.7 %copy-start.17 = (f32[1,32,1344]{2,0,1:T(1,128)S(1)}, f32[1,32,1344]{2,0,1:T(1,128)}, u32[]{:S(2)}) copy-start(f32[1,32,1344]{2,0,1:T(1,128)} %pad.167) | copy-start | bytes 516100
  245.4 32.8 %copy-start.18 = (f32[1,32,1344]{2,0,1:T(1,128)S(1)}, f32[1,32,1344]{2,0,1:T(1,128)}, u32[]{:S(2)}) copy-start(f32[1,32,1344]{2,0,1:T(1,128)} %pad.157) | copy-start | bytes 516100
  268.8 10.9 %copy-start.19 = (f32[1,32,1344]{2,0,1:T(1,128)S(1)}, f32[1,32,1344]{2,0,1:T(1,128)}, u32[]{:S(2)}) copy-start(f32[1,32,1344]{2,0,1:T(1,128)} %pad.147) | copy-start | bytes 516100
  268.8 10.9 %copy-start.20 = (f32[1,32,1344]{2,0,1:T(1,128)S(1)}, f32[1,32,1344]{2,0,1:T(1,128)}, u32[]{:S(2)}) copy-start(f32[1,32,1344]{2,0,1:T(1,128)} %pad.146) | copy-start | bytes 516100
  279.4 4.8 %copy-start.16 = (f32[1,32,1,1344]{3,1,2,0:T(8,128)S(1)}, f32[1,32,1,1344]{3,1,2,0:T(8,128)}, u32[]{:S(2)}) copy-start(f32[1,32,1,1344]{3,1,2,0:T(8,128)} %copy.115) | copy-start | bytes 516100
  279.4 4.8 %copy-start.30 = (f32[1344]{0:T(1024)S(1)}, f32[1344]{0:T(1024)}, u32[]{:S(2)}) copy-start(f32[1344]{0:T(1024)} %param.12) | copy-start | bytes 16132
  284.2 8.5 %copy-start.2 = (f32[1,256,1344]{2,1,0:T(8,128)S(1)}, f32[1,256,1344]{2,1,0:T(8,128)}, u32[]{:S(2)}) copy-start(f32[1,256,1344]{2,1,0:T(8,128)} %copy.77) | copy-start | bytes 4128772
  284.2 8.4 %copy-start.9 = (bf16[1,256,1344]{2,1,0:T(8,128)(2,1)S(1)}, bf16[1,256,1344]{2,1,0:T(8,128)(2,1)}, u32[]{:S(2)}) copy-start(bf16[1,256,1344]{2,1,0:T(8,128)(2,1)} %copy.78) | copy-start | bytes 2064388
  284.2 8.4 %copy-start.32 = (f32[1344]{0:T(1024)S(1)}, f32[1344]{0:T(1024)}, u32[]{:S(2)}) copy-start(f32[1344]{0:T(1024)} %param.13) | copy-start | bytes 16132
  291.5 1.1 copy-start.7
  292.7 3.6 copy-start.5
  298.9 1.4 copy-start.12
  304.1 1.2 copy-start.14
  306.9 3.1 copy-start.3
  306.9 3.1 copy-start.33
  310.0 5.5 %copy-start.34 = (f32[1344]{0:T(1024)S(1)}, f32[1344]{0:T(1024)}, u32[]{:S(2)}) copy-start(f32[1344]{0:T(1024)} %get-tuple-element.75) | copy-start | bytes 16132
  310.0 5.5 %copy-start.35 = (f32[1344]{0:T(1024)S(1)}, f32[1344]{0:T(1024)}, u32[]{:S(2)}) copy-start(f32[1344]{0:T(1024)} %get-tuple-element.80) | copy-start | bytes 16132
  310.0 5.5 %copy-start.36 = (f32[1344]{0:T(1024)S(1)}, f32[1344]{0:T(1024)}, u32[]{:S(2)}) copy-start(f32[1344]{0:T(1024)} %get-tuple-element.81) | copy-start | bytes 16132
  313.3 35.2 %copy-start.37 = (f32[1344]{0:T(1024)S(1)}, f32[1344]{0:T(1024)}, u32[]{:S(2)}) copy-start(f32[1344]{0:T(1024)} %param.14) | copy-start | bytes 16132
Sparse Core Ops, SparseCore 0:
  304.2 98.5 all-reduce.47
where the time goes:
time: 422 us; the launch traced here: 415 us
  local copies, waits for them, and re-layouts  187 us (44%)
  other arithmetic  109 us (26%)
  waiting for transfers between devices  53.7 us (13%)
  blocking collectives  40.5 us (10%)
  between operations  14.7 us (3%)
  matrix products  8.07 us (2%)
    pad x16, local copies, waits for them, and re-layouts, shards(): lax.associative_scan(combine, (group_prod, group_state), axis=1)  64.3 us
    psum x1, waiting for transfers between devices, shards(): lax.psum((local_a, local_x, bias_ga, bias_gx, decay_g), ('seq', 'dp'))  53.6 us
    pad x16, local copies, waits for them, and re-layouts, shards(): lax.associative_scan(combine, (group_prod, group_grad), reverse=True, axi...  53.6 us
    unnamed x98, local copies, waits for them, and re-layouts  41.1 us
    psum x1, blocking collectives, shards(): lax.psum((local_a, local_x, bias_ga, bias_gx, decay_g), ('seq', 'dp'))  33 us
    dot_general x1, other arithmetic, shards(): jnp.einsum('bntsc,bnsc->bntc', factor, drive.reshape(batch, groups, span_...  15.7 us
    add x10, other arithmetic, shards(): lax.associative_scan(combine, (group_prod, group_state), axis=1)  11.8 us
    add x10, other arithmetic, shards(): lax.associative_scan(combine, (group_prod, group_grad), reverse=True, axi...  10.7 us
  transfers between devices with their start and end apart: 2, of which 1 were waited for; matrix products, arithmetic and copies ran while one was open for 8% of the time, Pallas kernels for 0%

commit v1 on v0

--- a/solution.py
+++ b/solution.py
@@ -1,7 +1,17 @@
+import functools
 import jax
 import jax.numpy as jnp
 from jax import lax
 from jax.sharding import PartitionSpec as P
+
+
+def meet_the_slot(local, net_axis, across):
+    v_next = lax.psum(local, net_axis)
+    w1 = lax.psum(v_next, across)
+    return w1
+
+
+choose_yards = functools.partial(meet_the_slot, net_axis="dp", across="seq")
 
 
 def shifted(value, axis, steps):
@@ -124,8 +134,8 @@
     bias_ga = jnp.sum(dpre_a, (0, 1))
     bias_gx = jnp.sum(dpre_x, (0, 1))
     decay_g = jnp.sum(-8.0 * rate * wsum, (0, 1))
-    grad_a, grad_x, bias_ga, bias_gx, decay_g = lax.psum(
-        (local_a, local_x, bias_ga, bias_gx, decay_g), ("seq", "dp")
+    grad_a, grad_x, bias_ga, bias_gx, decay_g = choose_yards(
+        (local_a, local_x, bias_ga, bias_gx, decay_g)
     )
     return (input_grad, grad_a, grad_x, bias_ga, bias_gx, jax.nn.sigmoid(decay_param) * decay_g)
 

time: 422 us -> 510 us (1.21)
  waiting for transfers between devices: 53.7 us -> 155 us
  blocking collectives: 40.5 us -> 27.7 us
    psum x1 -> x2, waiting for transfers between devices: 53.6 us -> 155 us  [the longest x1 155 us: meet_the_slot(): v_next = lax.psum(local, net_axis)]
    psum x1 -> x2, blocking collectives: 33 us -> 20.2 us  [the longest x1 16.2 us: meet_the_slot(): v_next = lax.psum(local, net_axis)]
    unnamed x98 -> x100, local copies, waits for them, and re-layouts: 41.1 us -> 40.3 us
  transfers between devices with their start and end apart: 2 -> 3, of which waited for: 1 -> 1; matrix products, arithmetic and copies ran while one was open for 8% -> 7% of each run, Pallas kernels for 0% -> 0%
where the time goes in v1:
time: 510 us; the launch traced here: 504 us
  local copies, waits for them, and re-layouts  186 us (36%)
  waiting for transfers between devices  155 us (30%)
  other arithmetic  109 us (21%)
  blocking collectives  27.7 us (5%)
  between operations  14.7 us (3%)
  matrix products  8.04 us (2%)
    psum x1, waiting for transfers between devices, meet_the_slot(): v_next = lax.psum(local, net_axis)  155 us
    pad x16, local copies, waits for them, and re-layouts, shards(): lax.associative_scan(combine, (group_prod, group_state), axis=1)  64.3 us
    pad x16, local copies, waits for them, and re-layouts, shards(): lax.associative_scan(combine, (group_prod, group_grad), reverse=True, axi...  53.7 us
    unnamed x100, local copies, waits for them, and re-layouts  40.3 us
    psum x1, blocking collectives, meet_the_slot(): v_next = lax.psum(local, net_axis)  16.2 us
    dot_general x1, other arithmetic, shards(): jnp.einsum('bntsc,bnsc->bntc', factor, drive.reshape(batch, groups, span_...  15.7 us
    add x10, other arithmetic, shards(): lax.associative_scan(combine, (group_prod, group_state), axis=1)  11.8 us
    add x10, other arithmetic, shards(): lax.associative_scan(combine, (group_prod, group_grad), reverse=True, axi...  10.7 us
  transfers between devices with their start and end apart: 3, of which 1 were waited for; matrix products, arithmetic and copies ran while one was open for 7% of the time, Pallas kernels for 0%

profile of v1, /device:TPU:0, one launch (start us, length us, event | category | flops | bytes accessed | tf_op | source)
XLA Modules:
  0.0 503.6 jit_solution(14297077021866443657)
XLA Ops:
  8.6 3.0 collective-permute-start
  12.3 2.2 copy.78
  19.0 2.9 copy.77
  25.1 2.1 reshape.984
  28.7 6.4 %reduce_window_sum.23 = f32[1,32,8,1344]{3,2,1,0:T(8,128)S(1)} reduce-window(f32[1,32,8,1344]{3,2,1,0:T(8,128)} %divide_multiply_fusion, f32[]{:T(128)} %constant.20.clone.1), window={size=1x1x8x1 pad=0_0x0_0x7_0x0_0}, to_apply=%region_1.2 | reduce-window | flops 2408448 | bytes 2752516 | tf_op jit(solution)/shard_map/jit(cumsum)/reduce_window_sum | solution.py:78
  37.4 4.8 multiply_reduce_fusion.1
  48.1 15.7 %multiply_reduce_fusion = f32[32,1344,8]{1,2,0:T(8,128)S(1)} fusion(f32[32,1344,8]{1,2,0:T(8,128)S(1)} %fusion.6, f32[32,8,1344]{2,1,0:T(8,128)S(1)} %bitcast.112, pred[32,8,8]{2,1,0:T(8,128)(4,1)S(1)} %compare_and_fusion), kind=kLoop, calls=%fused_computation | loop fusion | flops 13418496 | bytes 4130816 | tf_op jit(solution)/shard_map/bntsc,bnsc->bntc/dot_general | solution.py:87
  74.7 1.9 pad.131
  87.3 3.2 pad.142
  91.8 3.2 pad.132
  95.0 3.2 pad.133
  98.2 3.2 pad.143
  117.2 1.9 pad.161
  120.4 1.9 pad.160
  127.9 3.2 pad.162
  132.4 3.2 pad.152
  135.6 3.2 pad.153
  138.8 3.2 pad.163
  147.9 4.7 pad.164
  154.0 4.7 pad.154
  158.7 4.7 pad.155
  163.4 4.7 pad.165
  169.7 2.0 fusion.34
  172.7 5.5 %pad.307 = f32[1,31,1344]{2,0,1:T(1,128)} pad(f32[1,16,1344]{2,0,1:T(1,128)S(1)} %add.530, f32[]{:T(128)} %constant.20.clone.1), padding=0_0_0x0_0_1x0_0_0 | pad | bytes 252676
  178.3 5.6 %pad.167 = f32[1,32,1344]{2,0,1:T(1,128)} pad(f32[1,16,1344]{2,0,1:T(1,128)S(1)} %add.530, f32[]{:T(128)} %constant.20.clone.1), padding=0_0_0x1_0_1x0_0_0 | pad | bytes 258052 | tf_op jit(solution)/shard_map/pad | solution.py:107
  183.8 8.5 %pad.305 = f32[1,31,1344]{2,0,1:T(1,128)} pad(f32[1,16,1344]{2,0,1:T(1,128)} %add.524, f32[]{:T(128)} %constant.20.clone.1), padding=0_0_0x0_0_1x0_0_0 | pad | bytes 252676
  192.3 8.4 %pad.157 = f32[1,32,1344]{2,0,1:T(1,128)} pad(f32[1,16,1344]{2,0,1:T(1,128)} %add.524, f32[]{:T(128)} %constant.20.clone.1), padding=0_0_0x1_0_1x0_0_0 | pad | bytes 258052 | tf_op jit(solution)/shard_map/pad | solution.py:107
  201.9 5.5 %pad.309 = f32[1,31,1344]{2,0,1:T(1,128)} pad(f32[1,16,1344]{2,0,1:T(1,128)S(1)} %add.496, f32[]{:T(128)} %constant.20.clone.1), padding=0_0_0x0_0_1x0_0_0 | pad | bytes 252676
  207.5 5.6 %pad.137 = f32[1,32,1344]{2,0,1:T(1,128)} pad(f32[1,16,1344]{2,0,1:T(1,128)S(1)} %add.496, f32[]{:T(128)} %constant.20.clone.1), padding=0_0_0x1_0_1x0_0_0 | pad | bytes 258052 | tf_op jit(solution)/shard_map/pad | solution.py:108
  214.0 4.7 pad.145
  219.7 5.5 %pad.311 = f32[1,31,1344]{2,0,1:T(1,128)} pad(f32[1,16,1344]{2,0,1:T(1,128)S(1)} %add.502, f32[]{:T(128)} %constant.20.clone.1), padding=0_0_0x0_0_1x0_0_0 | pad | bytes 252676
  225.2 5.6 %pad.147 = f32[1,32,1344]{2,0,1:T(1,128)} pad(f32[1,16,1344]{2,0,1:T(1,128)S(1)} %add.502, f32[]{:T(128)} %constant.20.clone.1), padding=0_0_0x1_0_1x0_0_0 | pad | bytes 258052 | tf_op jit(solution)/shard_map/pad | solution.py:108
  231.8 5.6 %pad.156 = f32[1,32,1344]{2,0,1:T(1,128)} pad(f32[1,16,1344]{2,0,1:T(1,128)S(1)} %pad_maximum_fusion.2, f32[]{:T(128)} %constant.20.clone.1), padding=0_0_0x0_1_1x0_0_0 | pad | bytes 258052 | tf_op jit(solution)/shard_map/pad | solution.py:107
  238.3 5.5 %pad.166 = f32[1,32,1344]{2,0,1:T(1,128)} pad(f32[1,16,1344]{2,0,1:T(1,128)S(1)} %pad_maximum_fusion.3, f32[]{:T(128)} %constant.20.clone.1), padding=0_0_0x0_1_1x0_0_0 | pad | bytes 258052 | tf_op jit(solution)/shard_map/pad | solution.py:107
  247.1 8.4 %pad.146 = f32[1,32,1344]{2,0,1:T(1,128)} pad(f32[1,16,1344]{2,0,1:T(1,128)} %pad_maximum_fusion.1, f32[]{:T(128)} %constant.20.clone.1), padding=0_0_0x0_1_1x0_0_0 | pad | bytes 258052 | tf_op jit(solution)/shard_map/pad | solution.py:108
  257.2 8.4 %pad.136 = f32[1,32,1344]{2,0,1:T(1,128)} pad(f32[1,16,1344]{2,0,1:T(1,128)} %pad_maximum_fusion, f32[]{:T(128)} %constant.20.clone.1), padding=0_0_0x0_1_1x0_0_0 | pad | bytes 258052 | tf_op jit(solution)/shard_map/pad | solution.py:108
  269.9 1.9 all_gather.12
  271.8 1.9 all_gather.13
  284.5 7.3 %fusion.15 = (f32[1344]{0:T(1024)}, f32[1,256,1344]{2,1,0:T(8,128)S(1)}, f32[1344]{0:T(1024)}, f32[1344]{0:T(1024)}, f32[1,256,1344]{2,1,0:T(8,128)}) fusion(bf16[1,256,1344]{2,1,0:T(8,128)(2,1)} %copy.78, f32[1,256,1344]{2,1,0:T(8,128)} %copy.77, f32[1344]{0:T(1024)} %param.13, f32[1344]{0:T(1024)S(1)} %fusion.19, f32[1,256,1344]{2,1,0:T(8,128)} %copy.75, ...), kind=kLoop, calls=%fused_computation.84 | loop fusion | flops 15134784 | bytes 10873600 | tf_op jit(solution)/shard_map/reduce_sum | solution.py:135
  294.3 2.2 copy.82
  296.5 2.7 fusion.8
  304.3 155.0 %all-reduce.51.cloned.1.call-done = (f32[4,336,336]{1,2,0:T(8,128)}, f32[4,336,336]{1,2,0:T(8,128)}) async-done(((f32[4,336,336]{1,2,0:T(8,128)}, f32[4,336,336]{1,2,0:T(8,128)}), (f32[4,336,336]{1,2,0:T(8,128)}, f32[4,336,336]{1,2,0:T(8,128)})) %all-reduce.51.cloned.1.call-update) | async-done | bytes 3612688 | tf_op jit(solution)/shard_map/psum | solution.py:9
  462.2 3.0 copy.83
  465.3 3.3 add_convert_fusion
  468.6 2.4 copy.84
  471.0 16.2 %all-reduce.44 = (f32[1344]{0:T(1024)S(1)}, f32[1344]{0:T(1024)S(1)}, f32[1344]{0:T(1024)S(1)}) all-reduce(f32[1344]{0:T(1024)S(1)} %copy-done.36, f32[1344]{0:T(1024)S(1)} %copy-done.35, f32[1344]{0:T(1024)S(1)} %copy-done.37), channel_id=1, replica_groups=mesh['seq'=2,'width'=4,'dp'=4] {'dp'}, use_global_device_ids=true, to_apply=%region_7.8 | all-reduce | flops 4032 | bytes 32256 | tf_op jit(solution)/shard_map/psum | solution.py:9
  487.3 4.0 all-reduce.46
  491.9 3.1 copy.85
  (214 shorter events, 113.7 us)
Async XLA Ops:
  7.2 9.0 %copy-start = (bf16[4,336,336]{2,1,0:T(8,128)(2,1)S(1)}, bf16[4,336,336]{2,1,0:T(8,128)(2,1)}, u32[]{:S(2)}) copy-start(bf16[4,336,336]{2,1,0:T(8,128)(2,1)} %param.10) | copy-start | bytes 2709508
  7.2 7.4 %copy-start.22 = (bf16[1,256,1344]{1,2,0:T(8,128)(2,1)S(1)}, bf16[1,256,1344]{1,2,0:T(8,128)(2,1)}, u32[]{:S(2)}) copy-start(bf16[1,256,1344]{1,2,0:T(8,128)(2,1)} %param.9) | copy-start | bytes 2064388
  7.2 452.2 %all-reduce.51.cloned.1.call-start = ((), (), s32[]{:S(2)}) async-start(), calls=%async_computation | async-start | bytes 8257536 | tf_op jit(solution)/shard_map/psum | solution.py:9
  8.6 27.3 %collective-permute-start = (s32[1,1]{1,0:T(1,128)}, s32[1,1]{1,0:T(1,128)}, u32[]{:S(2)}, u32[]{:S(2)}) collective-permute-start(s32[1,1]{1,0:T(1,128)} %slice.468), channel_id=1, source_target_pairs={{0,16},{1,17},{2,18},{3,19},{4,20},{5,21},{6,22},{7,23},{8,24},{9,... | collective-permute-start | bytes 20 | tf_op jit(solution)/shard_map/ppermute | solution.py:20
  14.6 1.6 copy-start.6
  16.1 1.2 copy-start.13
  25.1 2.1 copy-start.30
  28.7 7.3 %copy-start.42 = (s32[1,256]{1,0:T(1,128)S(1)}, s32[1,256]{1,0:T(1,128)}, u32[]{:S(2)}) copy-start(s32[1,256]{1,0:T(1,128)} %param.15) | copy-start | bytes 3076
  36.7 9.0 %copy-start.41 = (f32[1,256]{1,0:T(1,128)}, f32[1,256]{1,0:T(1,128)S(1)}, u32[]{:S(2)}) copy-start(f32[1,256]{1,0:T(1,128)S(1)} %get-tuple-element.83) | copy-start | bytes 3076
  37.4 9.1 %copy-start.1 = (f32[1,256,1344]{2,1,0:T(8,128)S(1)}, f32[1,256,1344]{2,1,0:T(8,128)}, u32[]{:S(2)}) copy-start(f32[1,256,1344]{2,1,0:T(8,128)} %copy.77) | copy-start | bytes 4128772
  37.4 9.1 %copy-start.4 = (f32[1,256,1344]{2,1,0:T(8,128)S(1)}, f32[1,256,1344]{2,1,0:T(8,128)}, u32[]{:S(2)}) copy-start(f32[1,256,1344]{2,1,0:T(8,128)} %copy.75) | copy-start | bytes 4128772
  37.4 9.1 %copy-start.32 = (f32[1344]{0:T(1024)S(1)}, f32[1344]{0:T(1024)}, u32[]{:S(2)}) copy-start(f32[1344]{0:T(1024)} %param.13) | copy-start | bytes 16132
  42.2 1.1 copy-start.10
  42.2 4.3 copy-start.8
  45.0 3.1 copy-start.16
  45.7 2.3 copy-start.43
  63.8 1.1 copy-start.11
  67.6 1.3 copy-start.23
  67.6 1.4 copy-start.24
  69.0 1.2 copy-start.25
  69.0 1.3 copy-start.26
  109.5 1.2 copy-start.27
  109.6 1.3 copy-start.28
  112.7 39.9 %copy-start.40 = (f32[1,1,1344]{2,0,1:T(1,128)S(1)}, f32[1,1,1344]{2,0,1:T(1,128)}, u32[]{:S(2)}) copy-start(f32[1,1,1344]{2,0,1:T(1,128)} %slice.512) | copy-start | bytes 16132
  171.7 30.0 %copy-start.29 = (f32[1,8,1344]{2,0,1:T(1,128)S(1)}, f32[1,8,1344]{2,0,1:T(1,128)}, u32[]{:S(2)}) copy-start(f32[1,8,1344]{2,0,1:T(1,128)} %add.494) | copy-start | bytes 129028
  171.7 41.4 %copy-start.39 = (f32[1,1,1344]{2,0,1:T(1,128)S(1)}, f32[1,1,1344]{2,0,1:T(1,128)}, u32[]{:S(2)}) copy-start(f32[1,1,1344]{2,0,1:T(1,128)} %slice.496) | copy-start | bytes 16132
  218.7 36.9 %slice-start = ((f32[1,32,1344]{2,0,1:T(1,128)}), f32[1,1,1344]{2,0,1:T(1,128)S(1)}, s32[]{:S(2)}) async-start(f32[1,32,1344]{2,0,1:T(1,128)} %copy-done.16), calls=%async_computation.2 | async-start | bytes 11264 | tf_op jit(solution)/shard_map/slice | solution.py:108
  245.7 31.7 %copy-start.18 = (f32[1,32,1344]{2,0,1:T(1,128)S(1)}, f32[1,32,1344]{2,0,1:T(1,128)}, u32[]{:S(2)}) copy-start(f32[1,32,1344]{2,0,1:T(1,128)} %pad.167) | copy-start | bytes 516100
  245.7 32.8 %copy-start.19 = (f32[1,32,1344]{2,0,1:T(1,128)S(1)}, f32[1,32,1344]{2,0,1:T(1,128)}, u32[]{:S(2)}) copy-start(f32[1,32,1344]{2,0,1:T(1,128)} %pad.157) | copy-start | bytes 516100
  269.1 10.9 %copy-start.20 = (f32[1,32,1344]{2,0,1:T(1,128)S(1)}, f32[1,32,1344]{2,0,1:T(1,128)}, u32[]{:S(2)}) copy-start(f32[1,32,1344]{2,0,1:T(1,128)} %pad.147) | copy-start | bytes 516100
  269.1 10.9 %copy-start.21 = (f32[1,32,1344]{2,0,1:T(1,128)S(1)}, f32[1,32,1344]{2,0,1:T(1,128)}, u32[]{:S(2)}) copy-start(f32[1,32,1344]{2,0,1:T(1,128)} %pad.146) | copy-start | bytes 516100
  279.6 4.8 copy-start.17
  279.6 4.8 copy-start.31
  284.5 8.4 %copy-start.2 = (f32[1,256,1344]{2,1,0:T(8,128)S(1)}, f32[1,256,1344]{2,1,0:T(8,128)}, u32[]{:S(2)}) copy-start(f32[1,256,1344]{2,1,0:T(8,128)} %copy.77) | copy-start | bytes 4128772
  284.5 8.4 %copy-start.9 = (bf16[1,256,1344]{2,1,0:T(8,128)(2,1)S(1)}, bf16[1,256,1344]{2,1,0:T(8,128)(2,1)}, u32[]{:S(2)}) copy-start(bf16[1,256,1344]{2,1,0:T(8,128)(2,1)} %copy.78) | copy-start | bytes 2064388
  284.5 8.4 %copy-start.33 = (f32[1344]{0:T(1024)S(1)}, f32[1344]{0:T(1024)}, u32[]{:S(2)}) copy-start(f32[1344]{0:T(1024)} %param.13) | copy-start | bytes 16132
  291.8 1.1 copy-start.7
  292.9 3.6 copy-start.5
  299.2 1.4 copy-start.12
  304.3 187.6 %all-reduce.53.cloned.1.call-start = ((), (), s32[]{:S(2)}) async-start(), calls=%async_computation.1 | async-start | bytes 8257536 | tf_op jit(solution)/shard_map/psum | solution.py:10
  459.4 1.2 copy-start.14
  462.2 3.0 copy-start.3
  462.2 3.0 copy-start.34
  465.2 5.8 %copy-start.35 = (f32[1344]{0:T(1024)S(1)}, f32[1344]{0:T(1024)}, u32[]{:S(2)}) copy-start(f32[1344]{0:T(1024)} %get-tuple-element.80) | copy-start | bytes 16132
  465.2 5.8 %copy-start.36 = (f32[1344]{0:T(1024)S(1)}, f32[1344]{0:T(1024)}, u32[]{:S(2)}) copy-start(f32[1344]{0:T(1024)} %get-tuple-element.85) | copy-start | bytes 16132
  465.3 5.8 %copy-start.37 = (f32[1344]{0:T(1024)S(1)}, f32[1344]{0:T(1024)}, u32[]{:S(2)}) copy-start(f32[1344]{0:T(1024)} %get-tuple-element.86) | copy-start | bytes 16132
  468.6 22.7 %copy-start.38 = (f32[1344]{0:T(1024)S(1)}, f32[1344]{0:T(1024)}, u32[]{:S(2)}) copy-start(f32[1344]{0:T(1024)} %param.14) | copy-start | bytes 16132
  491.9 3.1 copy-start.15
Sparse Core Ops, SparseCore 0:
  304.4 154.9 all-reduce.50
  462.0 27.2 all-reduce.52
